TPU v7x, 32 devices: a whole 2x2x4 slice. The times are simulated.
32 devices in a mesh: dp: 8 (over z, y), mp: 4 (over x, core).
Axes of the slice: x: 2, y: 2, z: 4, core: 2. Of those that a mesh axis runs over, the one named last changes fastest.
Arguments:
- hidden: bfloat16 [5632, 7168], P('dp', 'mp'), may hold values from -0.1875 to 0.1875
- router_weight: bfloat16 [7168, 256], P(('mp', 'dp')), may hold values from -3 to 3
- logits: float32 [5632, 256], P(('dp', 'mp')), may hold values from -12 to 240
- first_pot: float32 [256], replicated, may hold values from -1 to 1
- second_pot: float32 [256], replicated, may hold values from -1 to 1
- expert_index: int32 [5632], P(('dp', 'mp')), may hold values from 0 to 255
- loss_grad: float32 [5632], P(('dp', 'mp')), may hold values from -9 to 9
Outputs:
- weight_grad: float32 [7168, 256], P(('mp', 'dp'))
- hidden_grad: bfloat16 [5632, 7168], P('dp', 'mp')
All inputs are finite; a program needn't handle non-finite values.
Results may differ from a plain program's by a relative error of at most 0.005.
Values may be sent and summed in bfloat16 or wider, within the bound.
A program may use at most 64 MiB of HBM per device.

v0:
```python
import jax
import jax.numpy as jnp
from jax import lax
from jax.sharding import PartitionSpec as P


def neg_lse(values):
    top = jnp.max(values, axis=1, keepdims=True)
    return -(top[:, 0] + jnp.log(jnp.sum(jnp.exp(values - top), axis=1)))


def body(hidden, router_weight, logits, first_pot, second_pot, expert_index, loss_grad):
    experts = logits.shape[1]
    total_tokens = logits.shape[0] * lax.axis_size("dp") * lax.axis_size("mp")
    ratio = experts / total_tokens
    first_row = neg_lse(logits)
    first_soft = jnp.exp(logits + first_row[:, None])
    shifted = logits + first_pot[None, :]
    second_row = neg_lse(shifted)
    second_soft = jnp.exp(shifted + second_row[:, None])
    first_col = ratio * jnp.exp(logits + first_row[:, None] + first_pot[None, :])
    prob = jnp.exp(logits + second_row[:, None] + second_pot[None, :])
    second_col = ratio * prob
    onehot = (expert_index[:, None] == jnp.arange(experts, dtype=jnp.int32)[None, :]).astype(
        jnp.float32
    )
    direct = onehot * prob * loss_grad[:, None]
    row_direct = jnp.sum(direct, axis=1)
    second_colgrad = lax.psum(jnp.sum(direct, axis=0), ("dp", "mp"))
    second_rowgrad = row_direct - jnp.dot(
        second_col, second_colgrad, precision=lax.Precision.HIGHEST
    )
    first_colgrad = lax.psum(-jnp.sum(second_rowgrad[:, None] * second_soft, axis=0), ("dp", "mp"))
    first_rowgrad = -jnp.dot(first_col, first_colgrad, precision=lax.Precision.HIGHEST)
    score_grad = (
        direct
        - second_colgrad[None, :] * second_col
        - second_rowgrad[:, None] * second_soft
        - first_colgrad[None, :] * first_col
        - first_rowgrad[:, None] * first_soft
    ).astype(jnp.bfloat16)
    score_full = lax.all_gather(score_grad, "mp", axis=0, tiled=True)
    hidden_grad = lax.dot_general(
        score_full,
        lax.all_gather(router_weight, "dp", axis=0, tiled=True),
        (((1,), (1,)), ((), ())),
        preferred_element_type=jnp.float32,
    ).astype(jnp.bfloat16)
    weight_grad = lax.psum_scatter(
        lax.dot_general(
            hidden, score_full, (((0,), (0,)), ((), ())), preferred_element_type=jnp.float32
        ),
        "dp",
        scatter_dimension=0,
        tiled=True,
    )
    return (weight_grad, hidden_grad)


def solution(mesh):
    in_specs = (
        P("dp", "mp"),
        P(("mp", "dp"), None),
        P(("dp", "mp"), None),
        P(),
        P(),
        P(("dp", "mp")),
        P(("dp", "mp")),
    )
    out_specs = (P(("mp", "dp"), None), P("dp", "mp"))
    return jax.shard_map(body, mesh=mesh, in_specs=in_specs, out_specs=out_specs, check_vma=False)
```

profile of v0, /device:TPU:0, one launch (start us, length us, event | category | flops | bytes accessed | tf_op | source)
XLA Modules:
  0.0 188.7 jit_solution(2244073612009030590)
XLA Ops:
  7.2 0.0 copy-start
  7.2 0.0 reduce-scatter.4.cloned.1.call-start
  7.2 1.2 fusion.15
  8.4 1.2 exponential_reduce_fusion
  9.6 1.2 fusion.5
  10.8 42.0 %psum.14 = f32[256]{0:T(256)S(1)} all-reduce(f32[256]{0:T(256)S(1)} %get-tuple-element.6), channel_id=1, replica_groups=mesh['dp'=8,'mp'=4] {'dp','mp'}, use_global_device_ids=true, to_apply=%region_3.0 | all-reduce | flops 256 | bytes 2048 | tf_op jit(solution)/shard_map/psum | solution.py:29
  52.8 1.2 fusion.2
  54.1 0.1 sub.34
  54.1 1.1 fusion.7
  55.2 40.1 %psum.15 = f32[256]{0:T(256)S(1)} all-reduce(f32[256]{0:T(256)S(1)} %neg.22), channel_id=1, replica_groups=mesh['dp'=8,'mp'=4] {'dp','mp'}, use_global_device_ids=true, to_apply=%region_8.0 | all-reduce | flops 256 | bytes 2048 | tf_op jit(solution)/shard_map/psum | solution.py:33
  95.3 1.2 fusion
  96.6 1.2 subtract_convert_fusion
  97.8 7.1 %all_gather.6 = bf16[704,256]{1,0:T(8,128)(2,1)S(1)} all-gather(bf16[176,256]{1,0:T(8,128)(2,1)S(1)} %subtract_convert_fusion), channel_id=1, replica_groups=mesh['dp'=8,'mp'=4] {'mp'}, dimensions={0}, use_global_device_ids=true | all-gather | bytes 450560 | tf_op jit(solution)/shard_map/all_gather | solution.py:42
  104.9 0.0 copy-done
  104.9 2.1 %convolution_bitcast_fusion = f32[1792,256]{0,1:T(8,128)} fusion(bf16[704,256]{1,0:T(8,128)(2,1)S(1)} %all_gather.6, bf16[704,1792]{1,0:T(8,128)(2,1)S(1)} %copy-done), kind=kOutput, calls=%fused_computation.1 | convolution fusion | flops 645922816 | bytes 4718592 | tf_op jit(solution)/shard_map/dot_general | solution.py:50
  107.0 0.0 copy-start.1
  107.0 2.8 %copy.11 = f32[1792,256]{1,0:T(8,128)} copy(f32[1792,256]{0,1:T(8,128)} %convolution_bitcast_fusion) | data formatting | bytes 3670016
  109.8 0.0 reduce-scatter.4.cloned.1.call-update
  109.8 0.0 copy-done.1
  109.8 34.5 %all_gather.7 = bf16[1792,256]{1,0:T(8,128)(2,1)S(1)} all-gather(bf16[224,256]{1,0:T(8,128)(2,1)S(1)} %copy-done.1), channel_id=1, replica_groups=mesh['dp'=8,'mp'=4] {'dp'}, dimensions={0}, use_global_device_ids=true | all-gather | bytes 1032192 | tf_op jit(solution)/shard_map/all_gather | solution.py:45
  144.4 2.3 %convolution_convert_fusion = bf16[704,1792]{1,0:T(8,128)(2,1)} fusion(bf16[704,256]{1,0:T(8,128)(2,1)S(1)} %all_gather.6, bf16[1792,256]{1,0:T(8,128)(2,1)S(1)} %all_gather.7), kind=kOutput, calls=%fused_computation | convolution fusion | flops 647184384 | bytes 3801088 | tf_op jit(solution)/shard_map/dot_general | solution.py:43
  146.7 35.1 %reduce-scatter.4.cloned.1.call-done = f32[224,256]{1,0:T(8,128)} async-done(((f32[1792,256]{1,0:T(8,128)}), f32[224,256]{1,0:T(8,128)}) %reduce-scatter.4.cloned.1.call-update) | async-done | bytes 229392
  (6 shorter events, 0.0 us)
Async XLA Ops:
  7.2 97.7 %copy-start = (bf16[704,1792]{1,0:T(8,128)(2,1)S(1)}, bf16[704,1792]{1,0:T(8,128)(2,1)}, u32[]{:S(2)}) copy-start(bf16[704,1792]{1,0:T(8,128)(2,1)} %param.7) | copy-start | bytes 7569412
  7.2 174.7 %reduce-scatter.4.cloned.1.call-start = ((), (), s32[]{:S(2)}) async-start(), calls=%async_computation.1 | async-start | bytes 2064384
  107.0 2.8 %copy-start.1 = (bf16[224,256]{1,0:T(8,128)(2,1)S(1)}, bf16[224,256]{1,0:T(8,128)(2,1)}, u32[]{:S(2)}) copy-start(bf16[224,256]{1,0:T(8,128)(2,1)} %param.8) | copy-start | bytes 344068
Sparse Core Ops, SparseCore 0:
  110.0 71.8 reduce-scatter.3
where the time goes:
time: 189 us
  blocking collectives  124 us (66%)
  waiting for transfers between devices  35.1 us (19%)
  between operations  14.1 us (7%)
  matrix products  6.93 us (4%)
  other arithmetic  5.94 us (3%)
  local copies, waits for them, and re-layouts  2.81 us (1%)
    psum x1, blocking collectives, body(): second_colgrad = lax.psum(jnp.sum(direct, axis=0), ('dp', 'mp'))  42 us
    psum x1, blocking collectives, body(): lax.psum(-jnp.sum(second_rowgrad[:, None] * second_soft, axis=0), ('dp',...  40.1 us
    unnamed x2, waiting for transfers between devices  35.1 us
    all_gather x1, blocking collectives, body(): lax.all_gather(router_weight, 'dp', axis=0, tiled=True)  34.5 us
    all_gather x1, blocking collectives, body(): score_full = lax.all_gather(score_grad, 'mp', axis=0, tiled=True)  7.07 us
  transfers between devices with their start and end apart: 1, of which 1 were waited for; matrix products, arithmetic and copies ran while one was open for 1% of the time, Pallas kernels for 0%

commit v1 on v0

--- a/solution.py
+++ b/solution.py
@@ -26,7 +26,7 @@
     )
     direct = onehot * prob * loss_grad[:, None]
     row_direct = jnp.sum(direct, axis=1)
-    second_colgrad = lax.psum(jnp.sum(direct, axis=0), ("dp", "mp"))
+    second_colgrad = lax.psum(lax.psum(jnp.sum(direct, axis=0), "mp"), "dp")
     second_rowgrad = row_direct - jnp.dot(
         second_col, second_colgrad, precision=lax.Precision.HIGHEST
     )

time: 189 us -> 173 us (0.915)
  blocking collectives: 124 us -> 109 us
    psum x1 -> x2, blocking collectives: 42 us -> 30 us  [body(): second_colgrad = lax.psum(lax.psum(jnp.sum(direct, axis=0), 'mp'), 'dp')]
    psum x1, blocking collectives: 40.1 us -> 36.8 us  [body(): lax.psum(-jnp.sum(second_rowgrad[:, None] * second_soft, axis=0), ('dp',...]
where the time goes in v1:
time: 173 us
  blocking collectives  109 us (63%)
  waiting for transfers between devices  33.9 us (20%)
  between operations  14.1 us (8%)
  matrix products  6.93 us (4%)
  other arithmetic  5.94 us (3%)
  local copies, waits for them, and re-layouts  2.81 us (2%)
    psum x1, blocking collectives, body(): lax.psum(-jnp.sum(second_rowgrad[:, None] * second_soft, axis=0), ('dp',...  36.8 us
    all_gather x1, blocking collectives, body(): lax.all_gather(router_weight, 'dp', axis=0, tiled=True)  35.3 us
    unnamed x2, waiting for transfers between devices  33.9 us
    psum x2, blocking collectives, body(): second_colgrad = lax.psum(lax.psum(jnp.sum(direct, axis=0), 'mp'), 'dp')  30 us
    all_gather x1, blocking collectives, body(): score_full = lax.all_gather(score_grad, 'mp', axis=0, tiled=True)  7.07 us
  transfers between devices with their start and end apart: 1, of which 1 were waited for; matrix products, arithmetic and copies ran while one was open for 1% of the time, Pallas kernels for 0%

profile of v1, /device:TPU:0, one launch (start us, length us, event | category | flops | bytes accessed | tf_op | source)
XLA Modules:
  0.0 173.0 jit_solution(4859562874453502369)
XLA Ops:
  7.2 0.0 copy-start
  7.2 0.0 reduce-scatter.4.cloned.1.call-start
  7.2 1.2 fusion.15
  8.4 1.2 exponential_reduce_fusion
  9.6 1.2 fusion.5
  10.8 8.4 %psum.21 = f32[256]{0:T(256)S(1)} all-reduce(f32[256]{0:T(256)S(1)} %get-tuple-element.6), channel_id=1, replica_groups=mesh['dp'=8,'mp'=4] {'mp'}, use_global_device_ids=true, to_apply=%region_3.0 | all-reduce | flops 256 | bytes 2048 | tf_op jit(solution)/shard_map/psum | solution.py:29
  19.2 21.7 %psum.22 = f32[256]{0:T(256)S(1)} all-reduce(f32[256]{0:T(256)S(1)} %psum.21), channel_id=1, replica_groups=mesh['dp'=8,'mp'=4] {'dp'}, use_global_device_ids=true, to_apply=%region_4.0 | all-reduce | flops 256 | bytes 2048 | tf_op jit(solution)/shard_map/psum | solution.py:29
  40.9 1.2 fusion.2
  42.1 0.1 sub.34
  42.2 1.1 fusion.7
  43.2 36.8 %psum.23 = f32[256]{0:T(256)S(1)} all-reduce(f32[256]{0:T(256)S(1)} %neg.22), channel_id=1, replica_groups=mesh['dp'=8,'mp'=4] {'dp','mp'}, use_global_device_ids=true, to_apply=%region_9.0 | all-reduce | flops 256 | bytes 2048 | tf_op jit(solution)/shard_map/psum | solution.py:33
  80.1 1.2 fusion
  81.4 1.2 subtract_convert_fusion
  82.6 7.1 %all_gather.6 = bf16[704,256]{1,0:T(8,128)(2,1)S(1)} all-gather(bf16[176,256]{1,0:T(8,128)(2,1)S(1)} %subtract_convert_fusion), channel_id=1, replica_groups=mesh['dp'=8,'mp'=4] {'mp'}, dimensions={0}, use_global_device_ids=true | all-gather | bytes 450560 | tf_op jit(solution)/shard_map/all_gather | solution.py:42
  89.6 0.0 copy-done
  89.6 2.1 %convolution_bitcast_fusion = f32[1792,256]{0,1:T(8,128)} fusion(bf16[704,256]{1,0:T(8,128)(2,1)S(1)} %all_gather.6, bf16[704,1792]{1,0:T(8,128)(2,1)S(1)} %copy-done), kind=kOutput, calls=%fused_computation.1 | convolution fusion | flops 645922816 | bytes 4718592 | tf_op jit(solution)/shard_map/dot_general | solution.py:50
  91.8 0.0 copy-start.1
  91.8 2.8 %copy.11 = f32[1792,256]{1,0:T(8,128)} copy(f32[1792,256]{0,1:T(8,128)} %convolution_bitcast_fusion) | data formatting | bytes 3670016
  94.6 0.0 reduce-scatter.4.cloned.1.call-update
  94.6 0.0 copy-done.1
  94.6 35.3 %all_gather.7 = bf16[1792,256]{1,0:T(8,128)(2,1)S(1)} all-gather(bf16[224,256]{1,0:T(8,128)(2,1)S(1)} %copy-done.1), channel_id=1, replica_groups=mesh['dp'=8,'mp'=4] {'dp'}, dimensions={0}, use_global_device_ids=true | all-gather | bytes 1032192 | tf_op jit(solution)/shard_map/all_gather | solution.py:45
  129.9 2.3 %convolution_convert_fusion = bf16[704,1792]{1,0:T(8,128)(2,1)} fusion(bf16[704,256]{1,0:T(8,128)(2,1)S(1)} %all_gather.6, bf16[1792,256]{1,0:T(8,128)(2,1)S(1)} %all_gather.7), kind=kOutput, calls=%fused_computation | convolution fusion | flops 647184384 | bytes 3801088 | tf_op jit(solution)/shard_map/dot_general | solution.py:43
  132.2 33.9 %reduce-scatter.4.cloned.1.call-done = f32[224,256]{1,0:T(8,128)} async-done(((f32[1792,256]{1,0:T(8,128)}), f32[224,256]{1,0:T(8,128)}) %reduce-scatter.4.cloned.1.call-update) | async-done | bytes 229392
  (6 shorter events, 0.0 us)
Async XLA Ops:
  7.2 82.5 %copy-start = (bf16[704,1792]{1,0:T(8,128)(2,1)S(1)}, bf16[704,1792]{1,0:T(8,128)(2,1)}, u32[]{:S(2)}) copy-start(bf16[704,1792]{1,0:T(8,128)(2,1)} %param.7) | copy-start | bytes 7569412
  7.2 159.0 %reduce-scatter.4.cloned.1.call-start = ((), (), s32[]{:S(2)}) async-start(), calls=%async_computation.1 | async-start | bytes 2064384
  91.8 2.8 %copy-start.1 = (bf16[224,256]{1,0:T(8,128)(2,1)S(1)}, bf16[224,256]{1,0:T(8,128)(2,1)}, u32[]{:S(2)}) copy-start(bf16[224,256]{1,0:T(8,128)(2,1)} %param.8) | copy-start | bytes 344068
Sparse Core Ops, SparseCore 0:
  94.7 71.3 reduce-scatter.3
